TPU v7x, 32 devices: a whole 2x2x4 slice. The times are simulated.
32 devices in a mesh: dp: 4 (over x, core), vocab: 8 (over z, y).
Axes of the slice: x: 2, y: 2, z: 4, core: 2. Of those that a mesh axis runs over, the one named last changes fastest.
Arguments:
- hidden: bfloat16 [1024, 2048], P('dp', 'vocab'), may hold values from -30 to 30
- table: bfloat16 [16000, 2048], P('vocab'), may hold values from -20 to 20
- targets: int32 [1024], P('dp'), may hold values from 0 to 15999
- input_ids: int32 [2048], P(('dp', 'vocab')), may hold values from 0 to 15999, as said below
- cotangent: bfloat16 [2048, 2048], P(('dp', 'vocab')), may hold values from -0.4375 to 0.4375
Outputs:
- token_loss: float32 [1024], P('dp')
- hidden_grad: bfloat16 [1024, 2048], P('dp', 'vocab')
- table_grad: bfloat16 [16000, 2048], P('vocab', 'dp')
Inputs may be any that keep to these rules, and one draw needn't show every extreme that they name: `input_ids`: within the 64 rows of one device, at most 16 ids fall in any one block of 2000 consecutive ids (the rows of one index of vocab); in every draw some block receives exactly 16 ids from every device.
All inputs are finite; a program needn't handle non-finite values.
Results may differ from a plain program's by a relative error of at most 0.0034.
Values may be sent and summed in bfloat16 or wider, within the bound.
A program may use at most 128 MiB of HBM per device.

v0:
```python
import jax
import jax.numpy as jnp
from jax import lax
from jax.sharding import PartitionSpec as P


def body(hidden, table, targets, input_ids, cotangent):
    vocab_rows = table.shape[0]
    model_width = table.shape[1]
    data_count = lax.axis_size("dp")
    vocab_count = lax.axis_size("vocab")
    first_row = lax.axis_index("vocab") * vocab_rows
    hidden_full = lax.all_gather(hidden, "vocab", axis=1, tiled=True)
    logits = lax.dot_general(
        hidden_full, table, (((1,), (1,)), ((), ())), preferred_element_type=jnp.float32
    )
    columns = lax.broadcasted_iota(jnp.int32, logits.shape, 1)
    is_target = columns == (targets - first_row)[:, None]
    picked = jnp.sum(jnp.where(is_target, logits, 0.0), axis=1)
    local_max = jnp.max(logits, axis=1)
    row_max = lax.pmax(local_max, "vocab")
    shifted = jnp.exp(logits - row_max[:, None])
    row_sum, target_logit = lax.psum((jnp.sum(shifted, axis=1), picked), "vocab")
    token_loss = row_max + jnp.log(row_sum) - target_logit
    residual = (shifted / row_sum[:, None] - jnp.where(is_target, 1.0, 0.0)).astype(jnp.bfloat16)
    hidden_part = jnp.dot(residual, table, preferred_element_type=jnp.float32)
    hidden_grad = lax.psum_scatter(hidden_part, "vocab", scatter_dimension=1, tiled=True).astype(
        jnp.bfloat16
    )
    row_count = input_ids.shape[0]
    capacity = max(2, 2 * row_count // vocab_count)
    slot_total = vocab_count * capacity
    owners = input_ids // vocab_rows
    offsets = input_ids - owners * vocab_rows
    later_rows = lax.broadcasted_iota(jnp.int32, (row_count, row_count), 0)
    earlier_rows = lax.broadcasted_iota(jnp.int32, (row_count, row_count), 1)
    earlier = (owners[:, None] == owners[None, :]) & (earlier_rows < later_rows)
    position = jnp.sum(earlier.astype(jnp.int32), axis=1)
    slot_index = owners * capacity + position
    selector = lax.broadcasted_iota(jnp.int32, (slot_total, row_count), 0) == slot_index[None, :]
    send_rows = jnp.dot(
        selector.astype(jnp.bfloat16), cotangent, preferred_element_type=jnp.float32
    ).astype(jnp.bfloat16)
    send_rows = send_rows.reshape(vocab_count, capacity, model_width)
    send_offsets = jnp.sum(jnp.where(selector, offsets[None, :] + 1, 0), axis=1) - 1
    offset_copies = jnp.broadcast_to(
        send_offsets.reshape(vocab_count, capacity, 1), (vocab_count, capacity, data_count)
    )
    got_rows, got_offsets = (
        lax.all_to_all(
            lax.all_to_all(send_rows, "dp", split_axis=2, concat_axis=1, tiled=True),
            "vocab",
            split_axis=0,
            concat_axis=0,
            tiled=True,
        ),
        lax.all_to_all(
            lax.all_to_all(offset_copies, "dp", split_axis=2, concat_axis=1, tiled=True),
            "vocab",
            split_axis=0,
            concat_axis=0,
            tiled=True,
        ),
    )
    block_width = model_width // data_count
    flat_rows = got_rows.reshape(-1, block_width)
    flat_offsets = got_offsets.reshape(-1)
    matches = (
        lax.broadcasted_iota(jnp.int32, (vocab_rows, flat_offsets.shape[0]), 0)
        == flat_offsets[None, :]
    )
    start_sum = jnp.dot(matches.astype(jnp.bfloat16), flat_rows, preferred_element_type=jnp.float32)
    hidden_block = lax.all_to_all(hidden_full, "dp", split_axis=1, concat_axis=0, tiled=True)
    table_sum = start_sum + lax.dot_general(
        lax.all_gather(residual, "dp", axis=0, tiled=True),
        hidden_block,
        (((0,), (0,)), ((), ())),
        preferred_element_type=jnp.float32,
    )
    return (token_loss, hidden_grad, table_sum.astype(jnp.bfloat16))


def solution(mesh):
    placed = (
        P("dp", "vocab"),
        P("vocab", None),
        P("dp"),
        P(("dp", "vocab")),
        P(("dp", "vocab"), None),
    )
    return jax.shard_map(
        body,
        mesh=mesh,
        in_specs=placed,
        out_specs=(P("dp"), P("dp", "vocab"), P("vocab", "dp")),
        check_vma=False,
    )
```

profile of v0, /device:TPU:0, one launch (start us, length us, event | category | flops | bytes accessed | tf_op | source)
XLA Modules:
  0.0 228.6 jit_solution(13817739331604094054)
XLA Ops:
  7.2 0.0 copy-start
  7.2 0.0 all-gather.3.cloned.1.call-start
  7.2 1.7 copy.18
  8.9 0.0 all-gather.3.cloned.1.call-update
  8.9 0.0 reduce-scatter.2.cloned.1.call-start
  9.0 0.7 broadcast_subtract_fusion
  9.7 44.0 %all-gather.3.cloned.1.call-done = bf16[256,2048]{0,1:T(8,128)(2,1)} async-done(((bf16[256,256]{0,1:T(8,128)(2,1)}), bf16[256,2048]{0,1:T(8,128)(2,1)}) %all-gather.3.cloned.1.call-update) | async-done | bytes 1048592 | tf_op jit(solution)/shard_map/all_gather | solution.py:13
  53.7 5.9 %fusion.5 = (f32[256]{0:T(256)S(1)}, f32[256,2000]{0,1:T(8,128)S(1)}) fusion(bf16[2000,2048]{1,0:T(8,128)(2,1)} %param.6, bf16[256,2048]{0,1:T(8,128)(2,1)} %all-gather.3.cloned.1.call-done), kind=kOutput, calls=%fused_computation.22 | convolution fusion | flops 2097663744 | bytes 11289600 | tf_op jit(solution)/shard_map/dot_general | solution.py:14
  59.6 19.2 %pmax.7 = f32[256]{0:T(256)S(1)} all-reduce(f32[256]{0:T(256)S(1)} %get-tuple-element.9), channel_id=1, replica_groups=mesh['dp'=4,'vocab'=8] {'vocab'}, use_global_device_ids=true, to_apply=%region_1.2 | all-reduce | flops 256 | bytes 2048 | tf_op jit(solution)/shard_map/pmax | solution.py:21
  78.7 0.6 fusion.2
  79.3 17.1 %all-reduce = (f32[256]{0:T(256)S(1)}, f32[256]{0:T(256)S(1)}) all-reduce(f32[256]{0:T(256)S(1)} %get-tuple-element.4, f32[256]{0:T(256)S(1)} %get-tuple-element.3), channel_id=1, replica_groups=mesh['dp'=4,'vocab'=8] {'vocab'}, use_global_device_ids=true, to_apply=%region_5.6 | all-reduce | flops 512 | bytes 4096 | tf_op jit(solution)/shard_map/psum | solution.py:23
  96.4 0.6 subtract_convert_fusion
  97.0 0.0 copy-start.1
  97.0 7.4 %fusion.6 = f32[256,2048]{1,0:T(8,128)} fusion(bf16[256,2000]{0,1:T(8,128)(2,1)S(1)} %subtract_convert_fusion, bf16[2000,2048]{1,0:T(8,128)(2,1)} %param.6), kind=kOutput, calls=%fused_computation.25 | convolution fusion | flops 2097152000 | bytes 11313152 | tf_op jit(solution)/shard_map/dot_general | solution.py:26
  104.4 0.0 copy-done.1
  104.4 0.0 copy-start.2
  104.4 0.0 reduce-scatter.2.cloned.1.call-update
  104.5 0.0 all-gather.5.cloned.1.call-start
  104.5 0.7 all-gather.5.cloned.1.call-update
  105.2 0.0 copy-done.2
  105.2 0.2 convert_reduce_fusion
  105.4 0.1 select_reduce_fusion.1
  105.5 0.1 sub.44
  105.6 0.7 reshape.45
  106.3 3.2 %all-to-all-start = ((s32[4,1,128]{2,1,0:T(1,128)}), s32[4,1,128]{2,1,0:T(1,128)S(1)}, u32[]{:S(2)}, u32[]{:S(2)}) async-start(s32[4,1,128]{2,1,0:T(1,128)} %reshape.45), calls=%async_computation.1 | async-start | bytes 4096 | tf_op jit(solution)/shard_map/all_to_all | solution.py:58
  109.5 0.0 copy-done
  109.5 0.4 convolution_convert_fusion
  109.9 4.2 %copy.21 = bf16[8,16,2048]{1,0,2:T(8,128)(2,1)} copy(bf16[8,16,2048]{2,1,0:T(8,128)(2,1)S(1)} %bitcast.33) | data formatting | bytes 1048576 | tf_op jit(solution)/shard_map/reshape | solution.py:44
  114.1 6.5 %reshape.43 = bf16[4,2,32768]{2,1,0:T(2,128)(2,1)} reshape(bf16[2048,8,16]{2,1,0:T(8,128)(2,1)} %bitcast.30) | data formatting | bytes 1048576
  120.6 0.0 all-to-all-done
  120.6 3.5 %all-to-all-start.2 = ((bf16[4,2,32768]{2,1,0:T(2,128)(2,1)}), bf16[4,2,32768]{2,1,0:T(2,128)(2,1)S(1)}, u32[]{:S(2)}, u32[]{:S(2)}) async-start(bf16[4,2,32768]{2,1,0:T(2,128)(2,1)} %reshape.43), calls=%async_computation.3 | async-start | bytes 1048576 | tf_op jit(solution)/shard_map/all_to_all | solution.py:51
  124.1 0.5 broadcast.29
  124.6 0.7 reduce.4
  125.3 0.1 reshape.46
  125.4 0.7 all_to_all.49
  126.0 6.8 %all-to-all-done.2 = bf16[4,2,32768]{2,1,0:T(2,128)(2,1)S(1)} async-done(((bf16[4,2,32768]{2,1,0:T(2,128)(2,1)}), bf16[4,2,32768]{2,1,0:T(2,128)(2,1)S(1)}, u32[]{:S(2)}, u32[]{:S(2)}) %all-to-all-start.2) | async-done | bytes 524320 | tf_op jit(solution)/shard_map/all_to_all | solution.py:51
  132.9 3.3 %all-to-all-start.1 = ((s32[8,64,1]{1,2,0:T(1,128)}), s32[8,64,1]{1,2,0:T(1,128)S(1)}, u32[]{:S(2)}, u32[]{:S(2)}) async-start(s32[8,64,1]{1,2,0:T(1,128)} %bitcast.2), calls=%async_computation.2 | async-start | bytes 8192 | tf_op jit(solution)/shard_map/all_to_all | solution.py:57
  136.2 4.1 %reshape.44 = bf16[2048,8,16]{2,1,0:T(8,128)(2,1)} reshape(bf16[4,2,32768]{2,1,0:T(2,128)(2,1)S(1)} %all-to-all-done.2) | data formatting | bytes 1048576
  140.3 4.9 %copy.25 = bf16[8,16,4,512]{3,2,1,0:T(4,128)(2,1)S(1)} copy(bf16[8,16,4,512]{1,0,3,2:T(8,128)(2,1)} %bitcast.31) | data formatting | bytes 1048576 | tf_op jit(solution)/shard_map/all_to_all | solution.py:51
  145.2 0.1 copy.23
  145.3 0.0 all-to-all-done.1
  145.3 27.8 %all_to_all.65 = bf16[8,64,512]{2,1,0:T(8,128)(2,1)S(1)} all-to-all(bf16[8,64,512]{2,1,0:T(8,128)(2,1)S(1)} %bitcast.35), channel_id=1, replica_groups=mesh['dp'=4,'vocab'=8] {'vocab'}, dimensions={0} | all-to-all | bytes 1048576 | tf_op jit(solution)/shard_map/all_to_all | solution.py:50
  173.1 3.7 %all-to-all-start.4 = ((bf16[256,4,512]{0,2,1:T(8,128)(2,1)}), bf16[256,4,512]{0,2,1:T(8,128)(2,1)S(1)}, u32[]{:S(2)}, u32[]{:S(2)}) async-start(bf16[256,4,512]{0,2,1:T(8,128)(2,1)} %bitcast.8), calls=%async_computation.5 | async-start | bytes 2097152 | tf_op jit(solution)/shard_map/all_to_all | solution.py:73
  176.8 0.5 broadcast.27
  177.3 0.7 reduce.3
  178.0 0.1 eq.46
  178.1 3.1 %fusion = f32[2000,512]{1,0:T(8,128)} fusion(bf16[512,512]{1,0:T(8,128)(2,1)S(1)} %bitcast.37, s32[512]{0:T(512)S(1)} %eq.46), kind=kOutput, calls=%fused_computation.2 | convolution fusion | flops 1049600000 | bytes 4622336 | tf_op jit(solution)/shard_map/dot_general | solution.py:72
  181.2 0.6 add_subtract_fusion
  181.8 14.4 %all-to-all-done.4 = bf16[256,4,512]{0,2,1:T(8,128)(2,1)S(1)} async-done(((bf16[256,4,512]{0,2,1:T(8,128)(2,1)}), bf16[256,4,512]{0,2,1:T(8,128)(2,1)S(1)}, u32[]{:S(2)}, u32[]{:S(2)}) %all-to-all-start.4) | async-done | bytes 1048608 | tf_op jit(solution)/shard_map/all_to_all | solution.py:73
  196.1 0.5 copy.24
  196.7 0.0 reduce-scatter.2.cloned.1.call-done
  196.7 1.6 convert_element_type.18
  198.3 16.8 %all-gather.5.cloned.1.call-done = bf16[1024,2000]{0,1:T(8,128)(2,1)} async-done(((bf16[256,2000]{0,1:T(8,128)(2,1)}), bf16[1024,2000]{0,1:T(8,128)(2,1)}) %all-gather.5.cloned.1.call-update) | async-done | bytes 4096016 | tf_op jit(solution)/shard_map/all_gather | solution.py:75
  215.1 7.0 %add_convert_fusion = bf16[2000,512]{1,0:T(8,128)(2,1)} fusion(f32[2000,512]{1,0:T(8,128)} %fusion, bf16[1024,2000]{0,1:T(8,128)(2,1)} %all-gather.5.cloned.1.call-done, bf16[1024,512]{1,0:T(8,128)(2,1)S(1)} %bitcast.36), kind=kOutput, calls=%fused_computation | convolution fusion | flops 2099200000 | bytes 11288576 | tf_op jit(solution)/shard_map/dot_general | solution.py:74
  (6 shorter events, 0.0 us)
Async XLA Ops:
  7.2 102.4 %copy-start = (bf16[64,2048]{1,0:T(8,128)(2,1)S(1)}, bf16[64,2048]{1,0:T(8,128)(2,1)}, u32[]{:S(2)}) copy-start(bf16[64,2048]{1,0:T(8,128)(2,1)} %param.9) | copy-start | bytes 786436
  7.2 46.5 %all-gather.3.cloned.1.call-start = ((), (), s32[]{:S(2)}) async-start(), calls=%async_computation.6 | async-start | bytes 1179648 | tf_op jit(solution)/shard_map/all_gather | solution.py:13
  8.9 187.8 %reduce-scatter.2.cloned.1.call-start = ((), (), s32[]{:S(2)}) async-start(), calls=%async_computation.7 | async-start | bytes 2359296 | tf_op jit(solution)/shard_map/reduce_scatter | solution.py:27
  97.0 7.4 %copy-start.1 = (bf16[256,2000]{0,1:T(8,128)(2,1)}, bf16[256,2000]{0,1:T(8,128)(2,1)S(1)}, u32[]{:S(2)}) copy-start(bf16[256,2000]{0,1:T(8,128)(2,1)S(1)} %subtract_convert_fusion) | copy-start | bytes 3072004
  104.4 0.8 copy-start.2
  104.5 110.7 %all-gather.5.cloned.1.call-start = ((), (), s32[]{:S(2)}) async-start(), calls=%async_computation.8 | async-start | bytes 5120000 | tf_op jit(solution)/shard_map/all_gather | solution.py:75
  106.3 14.3 %all-to-all-start = ((s32[4,1,128]{2,1,0:T(1,128)}), s32[4,1,128]{2,1,0:T(1,128)S(1)}, u32[]{:S(2)}, u32[]{:S(2)}) async-start(s32[4,1,128]{2,1,0:T(1,128)} %reshape.45), calls=%async_computation.1 | async-start | bytes 4096 | tf_op jit(solution)/shard_map/all_to_all | solution.py:58
  120.6 12.3 %all-to-all-start.2 = ((bf16[4,2,32768]{2,1,0:T(2,128)(2,1)}), bf16[4,2,32768]{2,1,0:T(2,128)(2,1)S(1)}, u32[]{:S(2)}, u32[]{:S(2)}) async-start(bf16[4,2,32768]{2,1,0:T(2,128)(2,1)} %reshape.43), calls=%async_computation.3 | async-start | bytes 1048576 | tf_op jit(solution)/shard_map/all_to_all | solution.py:51
  132.9 12.5 %all-to-all-start.1 = ((s32[8,64,1]{1,2,0:T(1,128)}), s32[8,64,1]{1,2,0:T(1,128)S(1)}, u32[]{:S(2)}, u32[]{:S(2)}) async-start(s32[8,64,1]{1,2,0:T(1,128)} %bitcast.2), calls=%async_computation.2 | async-start | bytes 8192 | tf_op jit(solution)/shard_map/all_to_all | solution.py:57
  173.1 23.0 %all-to-all-start.4 = ((bf16[256,4,512]{0,2,1:T(8,128)(2,1)}), bf16[256,4,512]{0,2,1:T(8,128)(2,1)S(1)}, u32[]{:S(2)}, u32[]{:S(2)}) async-start(bf16[256,4,512]{0,2,1:T(8,128)(2,1)} %bitcast.8), calls=%async_computation.5 | async-start | bytes 2097152 | tf_op jit(solution)/shard_map/all_to_all | solution.py:73
Sparse Core Ops, SparseCore 0:
  10.7 42.9 all-gather.2
  104.6 70.6 reduce-scatter.1
  177.4 37.6 all-gather.4
where the time goes:
time: 229 us
  waiting for transfers between devices  82.8 us (36%)
  blocking collectives  64 us (28%)
  local copies, waits for them, and re-layouts  24.7 us (11%)
  matrix products  23.8 us (10%)
  between operations  13.9 us (6%)
  starting transfers between devices  13.8 us (6%)
  other arithmetic  5.64 us (2%)
    all_gather x1, waiting for transfers between devices, body(): hidden_full = lax.all_gather(hidden, 'vocab', axis=1, tiled=True)  44 us
    all_to_all x1, blocking collectives, body(): lax.all_to_all(lax.all_to_all(send_rows, 'dp', split_axis=2, concat_axis=...  27.8 us
    pmax x1, blocking collectives, body(): row_max = lax.pmax(local_max, 'vocab')  19.2 us
    psum x1, blocking collectives, body(): lax.psum((jnp.sum(shifted, axis=1), picked), 'vocab')  17.1 us
    all_gather x1, waiting for transfers between devices, body(): lax.all_gather(residual, 'dp', axis=0, tiled=True)  16.8 us
    all_to_all x1, waiting for transfers between devices, body(): lax.all_to_all(hidden_full, 'dp', split_axis=1, concat_axis=0, tiled=True)  14.4 us
    unnamed x12, local copies, waits for them, and re-layouts  13.1 us
    dot_general x1, matrix products, body(): hidden_part = jnp.dot(residual, table, preferred_element_type=jnp.float32)  7.42 us
  transfers between devices with their start and end apart: 7, of which 4 were waited for; matrix products, arithmetic and copies ran while one was open for 13% of the time, Pallas kernels for 0%

commit v1 on v0

v1 whole, which is shorter than its diff:
```python
import functools

import jax
import jax.numpy as jnp
from jax import lax
from jax.experimental import pallas as pl
from jax.experimental.pallas import tpu as pltpu
from jax.sharding import PartitionSpec as P

MESH = pl.DeviceIdType.MESH
VMEM_LIMIT = 58 * 1024 * 1024


def remote(src, dst, send_sem, recv_sem, device):
    return pltpu.make_async_remote_copy(
        src_ref=src,
        dst_ref=dst,
        send_sem=send_sem,
        recv_sem=recv_sem,
        device_id=device,
        device_id_type=MESH,
    )


def greet(devices):
    barrier = pltpu.get_barrier_semaphore()
    for device in devices:
        pl.semaphore_signal(barrier, inc=1, device_id=device, device_id_type=MESH)
    pl.semaphore_wait(barrier, len(devices))


def gather_kernel(
    n_d, n_v, own_ref, full_ref, block_ref, local_sem, own_sem,
    send_sem, recv_sem, pass_sem, got_sem, block_send, block_recv,
):
    d = lax.axis_index("dp")
    v = lax.axis_index("vocab")
    half = n_v // 2
    per = n_v // n_d
    partner = v + 1 - 2 * lax.rem(v, 2)

    def same(step):
        return lax.rem(v + 2 * step, n_v)

    def across(step):
        return lax.rem(partner + 2 * step, n_v)

    devices = [(d, same(s)) for s in range(1, half)] + [(d, partner)]
    devices += [(lax.rem(d + t, n_d), v) for t in range(1, n_d)]
    greet(devices)

    started = []
    directs = []
    for s in range(1, half):
        copy = remote(own_ref, full_ref.at[v], send_sem.at[s], recv_sem.at[s], (d, same(s)))
        copy.start()
        directs.append(copy)
    local = pltpu.make_async_copy(own_ref, full_ref.at[v], local_sem)
    local.start()

    def relay(step, index, source):
        copy = remote(source, full_ref.at[index], pass_sem.at[step], got_sem.at[step], (d, partner))
        copy.start()
        started.append(copy)

    sends = []

    def to_block(slot, index, source):
        owner = index // per
        place = index - owner * per
        shift = lax.rem(owner - d + n_d, n_d)
        away = owner != d
        out = remote(
            source,
            block_ref.at[d, place],
            block_send.at[slot],
            block_recv.at[shift, place],
            (owner, v),
        )
        keep = pltpu.make_async_copy(source, block_ref.at[d, place], own_sem.at[slot])

        @pl.when(away)
        def _():
            out.start()

        @pl.when(jnp.logical_not(away))
        def _():
            keep.start()

        sends.append((away, out, keep))

    relay(0, v, own_ref)
    to_block(0, v, own_ref)
    for s in range(1, half):
        index = lax.rem(v - 2 * s + 2 * n_v, n_v)
        directs[s - 1].wait_recv()
        relay(s, index, full_ref.at[index])
        to_block(s, index, full_ref.at[index])
    for s in range(half):
        index = lax.rem(partner - 2 * s + 2 * n_v, n_v)
        started[s].wait_recv()
        to_block(half + s, index, full_ref.at[index])
    local.wait()
    for away, out, keep in sends:

        @pl.when(away)
        def _():
            out.wait_send()

        @pl.when(jnp.logical_not(away))
        def _():
            keep.wait()

    for copy in directs + started:
        copy.wait_send()
    for t in range(1, n_d):
        source = lax.rem(d - t + n_d, n_d)
        for place in range(per):
            remote(
                own_ref, block_ref.at[source, place], block_send.at[0],
                block_recv.at[t, place], (source, v),
            ).wait_recv()


def gather(hidden, n_d, n_v):
    rows, width = hidden.shape
    half = n_v // 2
    per = n_v // n_d
    vmem = pl.BlockSpec(memory_space=pltpu.VMEM)
    return pl.pallas_call(
        functools.partial(gather_kernel, n_d, n_v),
        out_shape=(
            jax.ShapeDtypeStruct((n_v, rows, width), hidden.dtype),
            jax.ShapeDtypeStruct((n_d, per, rows, width), hidden.dtype),
        ),
        in_specs=[vmem],
        out_specs=(vmem, vmem),
        scratch_shapes=[
            pltpu.SemaphoreType.DMA,
            pltpu.SemaphoreType.DMA((n_v,)),
            pltpu.SemaphoreType.DMA((half,)),
            pltpu.SemaphoreType.DMA((half,)),
            pltpu.SemaphoreType.DMA((half,)),
            pltpu.SemaphoreType.DMA((half,)),
            pltpu.SemaphoreType.DMA((n_v,)),
            pltpu.SemaphoreType.DMA((n_d, per)),
        ],
        compiler_params=pltpu.CompilerParams(
            collective_id=0, has_side_effects=True, vmem_limit_bytes=VMEM_LIMIT
        ),
    )(hidden)


def stats_kernel(n_v, own_ref, all_ref, local_sem, send_sem, recv_sem):
    d = lax.axis_index("dp")
    v = lax.axis_index("vocab")
    greet([(d, lax.rem(v + s, n_v)) for s in range(1, n_v)])
    copies = []
    for s in range(1, n_v):
        copy = remote(
            own_ref, all_ref.at[v], send_sem.at[s], recv_sem.at[s], (d, lax.rem(v + s, n_v))
        )
        copy.start()
        copies.append(copy)
    local = pltpu.make_async_copy(own_ref, all_ref.at[v], local_sem)
    local.start()
    local.wait()
    for copy in copies:
        copy.wait()


def exchange_stats(stats, n_v):
    vmem = pl.BlockSpec(memory_space=pltpu.VMEM)
    return pl.pallas_call(
        functools.partial(stats_kernel, n_v),
        out_shape=jax.ShapeDtypeStruct((n_v,) + stats.shape, stats.dtype),
        in_specs=[vmem],
        out_specs=vmem,
        scratch_shapes=[
            pltpu.SemaphoreType.DMA,
            pltpu.SemaphoreType.DMA((n_v,)),
            pltpu.SemaphoreType.DMA((n_v,)),
        ],
        compiler_params=pltpu.CompilerParams(collective_id=1, has_side_effects=True),
    )(stats)


def final_kernel(
    n_d, n_v, reduces, res_ref, table_ref, rows_ref, ids_ref,
    grad_ref, all_ref, got_rows_ref, got_ids_ref,
    pair_out, pair_in, sums, cross_out, cross_in,
    local_sem, res_send, res_recv, pass_send, pass_recv,
    pair_send, pair_recv, cross_send, cross_recv,
    row_send, row_recv, id_send, id_recv,
):
    d = lax.axis_index("dp")
    v = lax.axis_index("vocab")
    half = n_v // 2
    half_d = n_d // 2
    mate = d + 1 - 2 * lax.rem(d, 2)
    partner = v + 1 - 2 * lax.rem(v, 2)
    total = n_d * n_v
    me = d * n_v + v

    def place(step):
        other = lax.rem(me + step, total)
        return other // n_v, lax.rem(other, n_v)

    greet([place(s) for s in range(1, total)])

    directs = []
    for s in range(1, half_d):
        copy = remote(
            res_ref, all_ref.at[d], res_send.at[s], res_recv.at[s], (lax.rem(d + 2 * s, n_d), v)
        )
        copy.start()
        directs.append(copy)
    passes = [remote(res_ref, all_ref.at[d], pass_send.at[0], pass_recv.at[0], (mate, v))]
    passes[0].start()
    locals_ = [
        pltpu.make_async_copy(res_ref, all_ref.at[d], local_sem.at[0]),
        pltpu.make_async_copy(rows_ref.at[d, v], got_rows_ref.at[d, v], local_sem.at[1]),
        pltpu.make_async_copy(ids_ref.at[v], got_ids_ref.at[d, v], local_sem.at[2]),
    ]
    for copy in locals_:
        copy.start()

    order = [(s + 1) % half for s in range(half)]
    width = table_ref.shape[1] // n_v

    def product(index):
        return jnp.dot(
            res_ref[...],
            table_ref[:, pl.ds(pl.multiple_of(index * width, 128), width)],
            preferred_element_type=jnp.float32,
        )

    pairs = {}
    if reduces:
        for s in order:
            pair_out[s] = product(lax.rem(partner + 2 * s, n_v))
            pairs[s] = remote(
                pair_out.at[s], pair_in.at[s], pair_send.at[s], pair_recv.at[s], (d, partner)
            )
            pairs[s].start()

    shuffles = []
    for s in range(1, total):
        to_d, to_v = place(s)
        for copy in (
            remote(
                rows_ref.at[to_d, to_v], got_rows_ref.at[d, v], row_send.at[s], row_recv.at[s],
                (to_d, to_v),
            ),
            remote(
                ids_ref.at[to_v], got_ids_ref.at[d, v], id_send.at[s], id_recv.at[s], (to_d, to_v)
            ),
        ):
            copy.start()
            shuffles.append(copy)

    crosses = []
    if reduces:
        for s in order:
            sums[s] = product(lax.rem(v + 2 * s, n_v))
        for s in order:
            pairs[s].wait_recv()
            if s == 0:
                continue
            cross_out[s] = (sums[s] + pair_in[s]).astype(jnp.bfloat16)
            copy = remote(
                cross_out.at[s], cross_in.at[s], cross_send.at[s], cross_recv.at[s],
                (d, lax.rem(v + 2 * s, n_v)),
            )
            copy.start()
            crosses.append(copy)

    for s in range(1, half_d):
        source = lax.rem(d - 2 * s + 2 * n_d, n_d)
        directs[s - 1].wait_recv()
        copy = remote(
            all_ref.at[source], all_ref.at[source], pass_send.at[s], pass_recv.at[s], (mate, v)
        )
        copy.start()
        passes.append(copy)

    if reduces:
        value = sums[0] + pair_in[0]
        for s, copy in zip(order, crosses):
            copy.wait_recv()
            value = value + cross_in[s].astype(jnp.float32)
        grad_ref[...] = value.astype(jnp.bfloat16)
    else:
        grad_ref[...] = jnp.zeros_like(grad_ref)

    for copy in locals_:
        copy.wait()
    for copy in passes:
        copy.wait()
    for copy in directs + crosses + list(pairs.values()):
        copy.wait_send()
    for copy in shuffles:
        copy.wait()


def finish(residual, table, send_rows, send_ids, n_d, n_v):
    rows = residual.shape[0]
    width = table.shape[1] // n_v
    reduces = width % 128 == 0
    half = n_v // 2
    total = n_d * n_v
    kept = width if reduces else 128
    slots = half if reduces else 1
    if not reduces:
        table = table[:8, :n_v * 128]
    vmem = pl.BlockSpec(memory_space=pltpu.VMEM)
    dma = pltpu.SemaphoreType.DMA
    results = pl.pallas_call(
        functools.partial(final_kernel, n_d, n_v, reduces),
        out_shape=(
            jax.ShapeDtypeStruct((rows, kept), jnp.bfloat16),
            jax.ShapeDtypeStruct((n_d,) + residual.shape, residual.dtype),
            jax.ShapeDtypeStruct(send_rows.shape, send_rows.dtype),
            jax.ShapeDtypeStruct((n_d,) + send_ids.shape, send_ids.dtype),
        ),
        in_specs=[vmem] * 4,
        out_specs=(vmem,) * 4,
        scratch_shapes=[
            pltpu.VMEM((slots, rows, kept), jnp.float32),
            pltpu.VMEM((slots, rows, kept), jnp.float32),
            pltpu.VMEM((slots, rows, kept), jnp.float32),
            pltpu.VMEM((slots, rows, kept), jnp.bfloat16),
            pltpu.VMEM((slots, rows, kept), jnp.bfloat16),
            dma((3,)),
            dma((n_d,)), dma((n_d,)), dma((n_d,)), dma((n_d,)),
            dma((half,)), dma((half,)), dma((half,)), dma((half,)),
            dma((total,)), dma((total,)), dma((total,)), dma((total,)),
        ],
        compiler_params=pltpu.CompilerParams(
            collective_id=2, has_side_effects=True, vmem_limit_bytes=VMEM_LIMIT
        ),
    )(residual, table, send_rows, send_ids)
    return reduces, results


def body(hidden, table, targets, input_ids, cotangent):
    vocab_rows, model_width = table.shape
    n_d = lax.axis_size("dp")
    n_v = lax.axis_size("vocab")
    tokens = hidden.shape[0]
    first_row = lax.axis_index("vocab") * vocab_rows
    block_width = model_width // n_d

    pieces, blocks = gather(hidden, n_d, n_v)
    hidden_full = jnp.transpose(pieces, (1, 0, 2)).reshape(tokens, model_width)
    hidden_block = jnp.transpose(blocks, (0, 2, 1, 3)).reshape(n_d * tokens, block_width)

    logits = lax.dot_general(
        hidden_full, table, (((1,), (1,)), ((), ())), preferred_element_type=jnp.float32
    )
    columns = lax.broadcasted_iota(jnp.int32, logits.shape, 1)
    is_target = columns == (targets - first_row)[:, None]
    picked = jnp.sum(jnp.where(is_target, logits, 0.0), axis=1)
    local_max = jnp.max(logits, axis=1)
    shifted = jnp.exp(logits - local_max[:, None])
    local_sum = jnp.sum(shifted, axis=1)
    stats = jnp.stack([local_max, local_sum, picked] + [picked] * 5)
    shared = exchange_stats(stats, n_v)
    maxima, sums = shared[:, 0], shared[:, 1]
    row_max = jnp.max(maxima, axis=0)
    row_sum = jnp.sum(sums * jnp.exp(maxima - row_max[None, :]), axis=0)
    target_logit = jnp.sum(shared[:, 2], axis=0)
    token_loss = row_max + jnp.log(row_sum) - target_logit
    residual = (
        jnp.exp(logits - row_max[:, None]) / row_sum[:, None] - jnp.where(is_target, 1.0, 0.0)
    ).astype(jnp.bfloat16)

    row_count = input_ids.shape[0]
    capacity = max(2, 2 * row_count // n_v)
    slot_total = n_v * capacity
    owners = input_ids // vocab_rows
    offsets = input_ids - owners * vocab_rows
    later_rows = lax.broadcasted_iota(jnp.int32, (row_count, row_count), 0)
    earlier_rows = lax.broadcasted_iota(jnp.int32, (row_count, row_count), 1)
    earlier = (owners[:, None] == owners[None, :]) & (earlier_rows < later_rows)
    position = jnp.sum(earlier.astype(jnp.int32), axis=1)
    slot_index = owners * capacity + position
    selector = lax.broadcasted_iota(jnp.int32, (slot_total, row_count), 0) == slot_index[None, :]
    packed = jnp.dot(
        selector.astype(jnp.bfloat16), cotangent, preferred_element_type=jnp.float32
    ).astype(jnp.bfloat16)
    send_rows = jnp.transpose(packed.reshape(n_v, capacity, n_d, block_width), (2, 0, 1, 3))
    send_offsets = jnp.sum(jnp.where(selector, offsets[None, :] + 1, 0), axis=1) - 1
    send_ids = jnp.pad(
        send_offsets.reshape(n_v, 1, capacity), ((0, 0), (0, 0), (0, 128 - capacity)),
        constant_values=-1,
    )

    reduces, (grad, res_all, got_rows, got_ids) = finish(
        residual, table, send_rows, send_ids, n_d, n_v
    )
    if reduces:
        hidden_grad = grad
    else:
        hidden_part = jnp.dot(residual, table, preferred_element_type=jnp.float32)
        hidden_grad = lax.psum_scatter(
            hidden_part, "vocab", scatter_dimension=1, tiled=True
        ).astype(jnp.bfloat16)

    flat_rows = got_rows.reshape(-1, block_width)
    flat_offsets = got_ids[:, :, 0, :capacity].reshape(-1)
    matches = (
        lax.broadcasted_iota(jnp.int32, (vocab_rows, flat_offsets.shape[0]), 0)
        == flat_offsets[None, :]
    )
    start_sum = jnp.dot(matches.astype(jnp.bfloat16), flat_rows, preferred_element_type=jnp.float32)
    table_sum = start_sum + lax.dot_general(
        res_all.reshape(n_d * tokens, vocab_rows),
        hidden_block,
        (((0,), (0,)), ((), ())),
        preferred_element_type=jnp.float32,
    )
    return (token_loss, hidden_grad, table_sum.astype(jnp.bfloat16))


def solution(mesh):
    placed = (
        P("dp", "vocab"),
        P("vocab", None),
        P("dp"),
        P(("dp", "vocab")),
        P(("dp", "vocab"), None),
    )
    return jax.shard_map(
        body,
        mesh=mesh,
        in_specs=placed,
        out_specs=(P("dp"), P("dp", "vocab"), P("vocab", "dp")),
        check_vma=False,
    )
```

time: 229 us -> 113 us (0.49)
  Pallas kernels: 0 us -> 84 us
  waiting for transfers between devices: 82.8 us -> 0 us
  blocking collectives: 64 us -> 0 us
  local copies, waits for them, and re-layouts: 24.7 us -> 9.85 us
  starting transfers between devices: 13.8 us -> 0 us
  between operations: 13.9 us -> 0.78 us
  matrix products: 23.8 us -> 12.2 us
    pallas_call x0 -> x3, Pallas kernels: none -> 84 us  [the longest x1 44.2 us: finish(): pl.pallas_call(functools.partial(final_kernel, n_d, n_v, reduces), out_sh...]
    all_gather x2 -> x0, waiting for transfers between devices: 60.8 us -> none  [the longest x1 44 us: body(): hidden_full = lax.all_gather(hidden, 'vocab', axis=1, tiled=True)]
    all_to_all x1 -> x0, blocking collectives: 27.8 us -> none  [body(): lax.all_to_all(lax.all_to_all(send_rows, 'dp', split_axis=2, concat_axis=...]
    all_to_all x4 -> x0, waiting for transfers between devices: 21.2 us -> none  [the longest x1 14.4 us: body(): lax.all_to_all(hidden_full, 'dp', split_axis=1, concat_axis=0, tiled=True)]
    pmax x1 -> x0, blocking collectives: 19.2 us -> none  [body(): row_max = lax.pmax(local_max, 'vocab')]
    psum x1 -> x0, blocking collectives: 17.1 us -> none  [body(): lax.psum((jnp.sum(shifted, axis=1), picked), 'vocab')]
    all_to_all x4 -> x0, starting transfers between devices: 13.7 us -> none  [the longest x1 3.7 us: body(): lax.all_to_all(hidden_full, 'dp', split_axis=1, concat_axis=0, tiled=True)]
    unnamed x12, local copies, waits for them, and re-layouts: 13.1 us -> 1.85 us
  transfers between devices with their start and end apart: 7 -> 0, of which waited for: 4 -> 0; matrix products, arithmetic and copies ran while one was open for 13% -> 0% of each run, Pallas kernels for 0% -> 0%
where the time goes in v1:
time: 113 us
  Pallas kernels  84 us (74%)
  matrix products  12.2 us (11%)
  local copies, waits for them, and re-layouts  9.85 us (9%)
  other arithmetic  5.71 us (5%)
    pallas_call x1, Pallas kernels, finish(): pl.pallas_call(functools.partial(final_kernel, n_d, n_v, reduces), out_sh...  44.2 us
    pallas_call x1, Pallas kernels, gather(): pl.pallas_call(functools.partial(gather_kernel, n_d, n_v), out_shape=(jax...  26.2 us
    pallas_call x1, Pallas kernels, exchange_stats(): pl.pallas_call(functools.partial(stats_kernel, n_v), out_shape=jax.ShapeD...  13.6 us
    dot_general x1, matrix products, body(): lax.dot_general(hidden_full, table, (((1,), (1,)), ((), ())), preferred_e...  5.74 us
    dot_general x1, matrix products, body(): lax.dot_general(res_all.reshape(n_d * tokens, vocab_rows), hidden_block,...  3.64 us
    dot_general x1, matrix products, body(): jnp.dot(matches.astype(jnp.bfloat16), flat_rows, preferred_element_type=j...  2.43 us

profile of v1, /device:TPU:0, one launch (start us, length us, event | category | flops | bytes accessed | tf_op | source)
XLA Modules:
  0.0 112.6 jit_solution(497748362515239820)
XLA Ops:
  0.6 0.0 copy-start
  0.6 0.7 broadcast_subtract_fusion
  1.4 0.7 subtract_add_fusion
  2.0 0.2 convert_reduce_fusion
  2.2 0.1 select_reduce_fusion.1
  2.3 0.1 sub.64
  2.4 0.6 pad.4.ids_ref
  3.0 0.0 copy-done
  3.0 0.4 convolution_convert_fusion
  3.4 0.4 reshape.46
  3.8 0.9 copy.41
  4.7 26.2 %shard_map.76 = (bf16[8,256,256]{2,1,0:T(8,128)(2,1)}, bf16[4,2,256,256]{3,2,1,0:T(8,128)(2,1)}) custom-call(bf16[256,256]{1,0:T(8,128)(2,1)} %own_ref.1), custom_call_target="tpu_custom_call" | custom-call | tf_op jit(solution)/shard_map/pallas_call | solution.py:130
  30.9 0.0 copy-start.2
  31.0 1.6 %copy.19 = bf16[256,8,256]{0,2,1:T(8,128)(2,1)S(1)} copy(bf16[256,8,256]{2,0,1:T(8,128)(2,1)} %bitcast.38) | data formatting | bytes 2097152 | tf_op jit(solution)/shard_map/transpose | solution.py:355
  32.5 0.0 copy-done.2
  32.5 1.1 copy.25
  33.6 0.2 copy.29
  33.9 5.7 %fusion.8 = (f32[256]{0:T(256)S(1)}, f32[256,2000]{0,1:T(8,128)S(1)}) fusion(bf16[2000,2048]{1,0:T(8,128)(2,1)} %table_ref.1, bf16[256,2048]{0,1:T(8,128)(2,1)S(1)} %bitcast.36), kind=kOutput, calls=%fused_computation.30 | convolution fusion | flops 2097663744 | bytes 11289600 | tf_op jit(solution)/shard_map/dot_general | solution.py:358
  39.6 0.0 copy-start.1
  39.6 0.4 exponential_reduce_fusion
  40.0 0.9 copy-done.1
  40.9 1.9 %copy.20 = f32[256,2000]{1,0:T(8,128)S(1)} copy(f32[256,2000]{0,1:T(8,128)} %copy-done.1) | data formatting | bytes 4096000 | tf_op jit(solution)/shard_map/dot_general | solution.py:358
  42.8 0.4 select_reduce_fusion
  43.2 0.6 stack.20.own_ref
  43.9 13.6 %shard_map.77 = f32[8,8,256]{2,1,0:T(8,128)} custom-call(f32[8,256]{1,0:T(8,128)} %stack.20.own_ref), custom_call_target="tpu_custom_call" | custom-call | tf_op jit(solution)/shard_map/pallas_call | solution.py:174
  57.4 1.0 slice_reduce_fusion.2
  58.5 1.7 %subtract_convert_fusion.res_ref = bf16[256,2000]{1,0:T(8,128)(2,1)} fusion(f32[256,2000]{1,0:T(8,128)S(1)} %copy.20, f32[256]{0:T(256)S(1)} %fusion.7, f32[256]{0:T(256)S(1)} %get-tuple-element.15, s32[256]{0:T(256)S(1)} %broadcast_subtract_fusion), kind=kLoop, calls=%fused_computation.4 | loop fusion | flops 3072000 | bytes 3075072 | tf_op jit(solution)/shard_map/convert_element_type | solution.py:376
  60.2 0.6 add_subtract_fusion
  60.7 44.2 %shard_map.78 = (bf16[256,256]{1,0:T(8,128)(2,1)}, bf16[4,256,2000]{2,1,0:T(8,128)(2,1)}, bf16[4,8,16,512]{3,2,1,0:T(8,128)(2,1)}, s32[4,8,1,128]{3,2,1,0:T(1,128)}) custom-call(bf16[256,2000]{1,0:T(8,128)(2,1)} %subtract_convert_fusion.res_ref, bf16[2000,2048]{1,0:T(8,128)(2,1)} %table_ref.1, bf16[4,8,16,512]{3,2,1,0:T(8,128)(2,1)} %bitcast.34, ...), custom_call_target="tpu_custom_call" | custom-call | tf_op jit(solution)/shard_map/pallas_call | solution.py:318
  105.0 0.8 slice_reduce_fusion
  105.7 0.1 eq.46
  105.8 0.0 copy-start.4
  105.8 2.4 %fusion = f32[2000,512]{1,0:T(8,128)S(1)} fusion(bf16[512,512]{1,0:T(8,128)(2,1)} %bitcast.49, s32[512]{0:T(512)S(1)} %eq.46), kind=kOutput, calls=%fused_computation.2 | convolution fusion | flops 1049600000 | bytes 4622336 | tf_op jit(solution)/shard_map/dot_general | solution.py:416
  108.3 0.0 copy-done.4
  108.3 0.0 copy-start.3
  108.3 3.6 %add_convert_fusion = bf16[2000,512]{1,0:T(8,128)(2,1)} fusion(f32[2000,512]{1,0:T(8,128)S(1)} %fusion, bf16[1024,2000]{1,0:T(8,128)(2,1)S(1)} %bitcast.48, bf16[1024,512]{1,0:T(8,128)(2,1)S(1)} %bitcast.35), kind=kOutput, calls=%fused_computation | convolution fusion | flops 2099200000 | bytes 11288576 | tf_op jit(solution)/shard_map/dot_general | solution.py:417
  111.9 0.0 copy-done.3
  111.9 0.7 copy.43
  (3 shorter events, 0.0 us)
Async XLA Ops:
  0.6 2.4 %copy-start = (bf16[64,2048]{1,0:T(8,128)(2,1)S(1)}, bf16[64,2048]{1,0:T(8,128)(2,1)}, u32[]{:S(2)}) copy-start(bf16[64,2048]{1,0:T(8,128)(2,1)} %param.9) | copy-start | bytes 786436
  30.9 1.6 %copy-start.2 = (bf16[4,2,256,256]{3,2,1,0:T(8,128)(2,1)S(1)}, bf16[4,2,256,256]{3,2,1,0:T(8,128)(2,1)}, u32[]{:S(2)}) copy-start(bf16[4,2,256,256]{3,2,1,0:T(8,128)(2,1)} %get-tuple-element.14) | copy-start | bytes 3145732
  39.6 1.3 %copy-start.1 = (f32[256,2000]{0,1:T(8,128)}, f32[256,2000]{0,1:T(8,128)S(1)}, u32[]{:S(2)}) copy-start(f32[256,2000]{0,1:T(8,128)S(1)} %get-tuple-element.22) | copy-start | bytes 6144004
  105.8 2.4 %copy-start.4 = (bf16[4,256,2000]{2,1,0:T(8,128)(2,1)S(1)}, bf16[4,256,2000]{2,1,0:T(8,128)(2,1)}, u32[]{:S(2)}) copy-start(bf16[4,256,2000]{2,1,0:T(8,128)(2,1)} %get-tuple-element.13) | copy-start | bytes 12288004
  108.3 3.6 %copy-start.3 = (bf16[256,256]{1,0:T(8,128)(2,1)S(1)}, bf16[256,256]{1,0:T(8,128)(2,1)}, u32[]{:S(2)}) copy-start(bf16[256,256]{1,0:T(8,128)(2,1)} %get-tuple-element.27) | copy-start | bytes 393220

commit v2 on v1

--- a/solution.py
+++ b/solution.py
@@ -39,11 +39,21 @@
     per = n_v // n_d
     partner = v + 1 - 2 * lax.rem(v, 2)
 
+    width = own_ref.shape[1]
+    aligned = width % 128 == 0
+
+    def piece(index):
+        if aligned:
+            return full_ref.at[:, pl.ds(pl.multiple_of(index * width, 128), width)]
+        return full_ref.at[index]
+
+    def part(group, spot):
+        if aligned:
+            return block_ref.at[group, :, pl.ds(pl.multiple_of(spot * width, 128), width)]
+        return block_ref.at[group, spot]
+
     def same(step):
         return lax.rem(v + 2 * step, n_v)
-
-    def across(step):
-        return lax.rem(partner + 2 * step, n_v)
 
     devices = [(d, same(s)) for s in range(1, half)] + [(d, partner)]
     devices += [(lax.rem(d + t, n_d), v) for t in range(1, n_d)]
@@ -52,14 +62,14 @@
     started = []
     directs = []
     for s in range(1, half):
-        copy = remote(own_ref, full_ref.at[v], send_sem.at[s], recv_sem.at[s], (d, same(s)))
+        copy = remote(own_ref, piece(v), send_sem.at[s], recv_sem.at[s], (d, same(s)))
         copy.start()
         directs.append(copy)
-    local = pltpu.make_async_copy(own_ref, full_ref.at[v], local_sem)
+    local = pltpu.make_async_copy(own_ref, piece(v), local_sem)
     local.start()
 
     def relay(step, index, source):
-        copy = remote(source, full_ref.at[index], pass_sem.at[step], got_sem.at[step], (d, partner))
+        copy = remote(source, piece(index), pass_sem.at[step], got_sem.at[step], (d, partner))
         copy.start()
         started.append(copy)
 
@@ -72,12 +82,12 @@
         away = owner != d
         out = remote(
             source,
-            block_ref.at[d, place],
+            part(d, place),
             block_send.at[slot],
             block_recv.at[shift, place],
             (owner, v),
         )
-        keep = pltpu.make_async_copy(source, block_ref.at[d, place], own_sem.at[slot])
+        keep = pltpu.make_async_copy(source, part(d, place), own_sem.at[slot])
 
         @pl.when(away)
         def _():
@@ -94,12 +104,12 @@
     for s in range(1, half):
         index = lax.rem(v - 2 * s + 2 * n_v, n_v)
         directs[s - 1].wait_recv()
-        relay(s, index, full_ref.at[index])
-        to_block(s, index, full_ref.at[index])
+        relay(s, index, piece(index))
+        to_block(s, index, piece(index))
     for s in range(half):
         index = lax.rem(partner - 2 * s + 2 * n_v, n_v)
         started[s].wait_recv()
-        to_block(half + s, index, full_ref.at[index])
+        to_block(half + s, index, piece(index))
     local.wait()
     for away, out, keep in sends:
 
@@ -117,7 +127,7 @@
         source = lax.rem(d - t + n_d, n_d)
         for place in range(per):
             remote(
-                own_ref, block_ref.at[source, place], block_send.at[0],
+                own_ref, part(source, place), block_send.at[0],
                 block_recv.at[t, place], (source, v),
             ).wait_recv()
 
@@ -126,12 +136,17 @@
     rows, width = hidden.shape
     half = n_v // 2
     per = n_v // n_d
+    full_shape = (n_v, rows, width)
+    block_shape = (n_d, per, rows, width)
+    if width % 128 == 0:
+        full_shape = (rows, n_v * width)
+        block_shape = (n_d, rows, per * width)
     vmem = pl.BlockSpec(memory_space=pltpu.VMEM)
     return pl.pallas_call(
         functools.partial(gather_kernel, n_d, n_v),
         out_shape=(
-            jax.ShapeDtypeStruct((n_v, rows, width), hidden.dtype),
-            jax.ShapeDtypeStruct((n_d, per, rows, width), hidden.dtype),
+            jax.ShapeDtypeStruct(full_shape, hidden.dtype),
+            jax.ShapeDtypeStruct(block_shape, hidden.dtype),
         ),
         in_specs=[vmem],
         out_specs=(vmem, vmem),
@@ -151,43 +166,10 @@
     )(hidden)
 
 
-def stats_kernel(n_v, own_ref, all_ref, local_sem, send_sem, recv_sem):
-    d = lax.axis_index("dp")
-    v = lax.axis_index("vocab")
-    greet([(d, lax.rem(v + s, n_v)) for s in range(1, n_v)])
-    copies = []
-    for s in range(1, n_v):
-        copy = remote(
-            own_ref, all_ref.at[v], send_sem.at[s], recv_sem.at[s], (d, lax.rem(v + s, n_v))
-        )
-        copy.start()
-        copies.append(copy)
-    local = pltpu.make_async_copy(own_ref, all_ref.at[v], local_sem)
-    local.start()
-    local.wait()
-    for copy in copies:
-        copy.wait()
-
-
-def exchange_stats(stats, n_v):
-    vmem = pl.BlockSpec(memory_space=pltpu.VMEM)
-    return pl.pallas_call(
-        functools.partial(stats_kernel, n_v),
-        out_shape=jax.ShapeDtypeStruct((n_v,) + stats.shape, stats.dtype),
-        in_specs=[vmem],
-        out_specs=vmem,
-        scratch_shapes=[
-            pltpu.SemaphoreType.DMA,
-            pltpu.SemaphoreType.DMA((n_v,)),
-            pltpu.SemaphoreType.DMA((n_v,)),
-        ],
-        compiler_params=pltpu.CompilerParams(collective_id=1, has_side_effects=True),
-    )(stats)
-
-
 def final_kernel(
-    n_d, n_v, reduces, res_ref, table_ref, rows_ref, ids_ref,
-    grad_ref, all_ref, got_rows_ref, got_ids_ref,
+    n_d, n_v, reduces, hid_ref, table_ref, target_ref, rows_ref, ids_ref,
+    loss_ref, grad_ref, all_ref, got_rows_ref, got_ids_ref,
+    logit_ref, res_ref, own_stats, all_stats, stat_local, stat_send, stat_recv,
     pair_out, pair_in, sums, cross_out, cross_in,
     local_sem, res_send, res_recv, pass_send, pass_recv,
     pair_send, pair_recv, cross_send, cross_recv,
@@ -208,6 +190,82 @@
 
     greet([place(s) for s in range(1, total)])
 
+    shuffles = []
+
+    def shuffle(first):
+        for s in range(first, total, 2):
+            to_d, to_v = place(s)
+            for copy in (
+                remote(
+                    rows_ref.at[to_d, to_v], got_rows_ref.at[d, v],
+                    row_send.at[s], row_recv.at[s], (to_d, to_v),
+                ),
+                remote(
+                    ids_ref.at[to_v], got_ids_ref.at[d, v],
+                    id_send.at[s], id_recv.at[s], (to_d, to_v),
+                ),
+            ):
+                copy.start()
+                shuffles.append(copy)
+
+    shuffle(1)
+    tokens, vocab_rows = res_ref.shape
+    target = target_ref[...]
+    chunks = [(c, min(256, vocab_rows - c)) for c in range(0, vocab_rows, 256)]
+
+    def hits(start, size):
+        return lax.broadcasted_iota(jnp.int32, (tokens, size), 1) + start == target
+
+    peak = jnp.full((tokens, 1), -jnp.inf, jnp.float32)
+    picked = jnp.zeros((tokens, 1), jnp.float32)
+    for start, size in chunks:
+        value = lax.dot_general(
+            hid_ref[...], table_ref[start:start + size, :], (((1,), (1,)), ((), ())),
+            preferred_element_type=jnp.float32,
+        )
+        logit_ref[:, start:start + size] = value
+        peak = jnp.maximum(peak, jnp.max(value, axis=1, keepdims=True))
+        picked = picked + jnp.sum(
+            jnp.where(hits(start, size), value, 0.0), axis=1, keepdims=True
+        )
+    amount = jnp.zeros((tokens, 1), jnp.float32)
+    for start, size in chunks:
+        value = jnp.exp(logit_ref[:, start:start + size] - peak)
+        logit_ref[:, start:start + size] = value
+        amount = amount + jnp.sum(value, axis=1, keepdims=True)
+    lane = lax.broadcasted_iota(jnp.int32, (tokens, 128), 1)
+    wide = jnp.where(lane == 0, peak, jnp.where(lane == 1, amount, picked))
+    own_stats[...] = jnp.transpose(wide)[:8]
+    stats = []
+    for s in range(1, n_v):
+        copy = remote(
+            own_stats, all_stats.at[v], stat_send.at[s], stat_recv.at[s],
+            (d, lax.rem(v + s, n_v)),
+        )
+        copy.start()
+        stats.append(copy)
+    keep_stats = pltpu.make_async_copy(own_stats, all_stats.at[v], stat_local)
+    keep_stats.start()
+    shuffle(2)
+    keep_stats.wait()
+    for copy in stats:
+        copy.wait()
+    row_max = all_stats[0, 0:1, :]
+    for k in range(1, n_v):
+        row_max = jnp.maximum(row_max, all_stats[k, 0:1, :])
+    row_sum = jnp.zeros_like(row_max)
+    target_logit = jnp.zeros_like(row_max)
+    for k in range(n_v):
+        row_sum = row_sum + all_stats[k, 1:2, :] * jnp.exp(all_stats[k, 0:1, :] - row_max)
+        target_logit = target_logit + all_stats[k, 2:3, :]
+    loss_ref[...] = row_max + jnp.log(row_sum) - target_logit
+    factor = jnp.exp(own_stats[0:1, :] - row_max) / row_sum
+    factor = jnp.transpose(jnp.broadcast_to(factor, (128, tokens)))[:, 0:1]
+    for start, size in chunks:
+        value = logit_ref[:, start:start + size] * factor
+        value = value - jnp.where(hits(start, size), 1.0, 0.0)
+        res_ref[:, start:start + size] = value.astype(jnp.bfloat16)
+
     directs = []
     for s in range(1, half_d):
         copy = remote(
@@ -243,21 +301,6 @@
                 pair_out.at[s], pair_in.at[s], pair_send.at[s], pair_recv.at[s], (d, partner)
             )
             pairs[s].start()
-
-    shuffles = []
-    for s in range(1, total):
-        to_d, to_v = place(s)
-        for copy in (
-            remote(
-                rows_ref.at[to_d, to_v], got_rows_ref.at[d, v], row_send.at[s], row_recv.at[s],
-                (to_d, to_v),
-            ),
-            remote(
-                ids_ref.at[to_v], got_ids_ref.at[d, v], id_send.at[s], id_recv.at[s], (to_d, to_v)
-            ),
-        ):
-            copy.start()
-            shuffles.append(copy)
 
     crosses = []
     if reduces:
@@ -303,29 +346,36 @@
         copy.wait()
 
 
-def finish(residual, table, send_rows, send_ids, n_d, n_v):
-    rows = residual.shape[0]
+def finish(hidden_full, table, target, send_rows, send_ids, n_d, n_v):
+    rows = hidden_full.shape[0]
+    vocab_rows = table.shape[0]
     width = table.shape[1] // n_v
     reduces = width % 128 == 0
     half = n_v // 2
     total = n_d * n_v
     kept = width if reduces else 128
     slots = half if reduces else 1
-    if not reduces:
-        table = table[:8, :n_v * 128]
     vmem = pl.BlockSpec(memory_space=pltpu.VMEM)
     dma = pltpu.SemaphoreType.DMA
     results = pl.pallas_call(
         functools.partial(final_kernel, n_d, n_v, reduces),
         out_shape=(
+            jax.ShapeDtypeStruct((1, rows), jnp.float32),
             jax.ShapeDtypeStruct((rows, kept), jnp.bfloat16),
-            jax.ShapeDtypeStruct((n_d,) + residual.shape, residual.dtype),
+            jax.ShapeDtypeStruct((n_d, rows, vocab_rows), jnp.bfloat16),
             jax.ShapeDtypeStruct(send_rows.shape, send_rows.dtype),
             jax.ShapeDtypeStruct((n_d,) + send_ids.shape, send_ids.dtype),
         ),
-        in_specs=[vmem] * 4,
-        out_specs=(vmem,) * 4,
+        in_specs=[vmem] * 5,
+        out_specs=(vmem,) * 5,
         scratch_shapes=[
+            pltpu.VMEM((rows, vocab_rows), jnp.float32),
+            pltpu.VMEM((rows, vocab_rows), jnp.bfloat16),
+            pltpu.VMEM((8, rows), jnp.float32),
+            pltpu.VMEM((n_v, 8, rows), jnp.float32),
+            dma,
+            dma((n_v,)),
+            dma((n_v,)),
             pltpu.VMEM((slots, rows, kept), jnp.float32),
             pltpu.VMEM((slots, rows, kept), jnp.float32),
             pltpu.VMEM((slots, rows, kept), jnp.float32),
@@ -337,9 +387,9 @@
             dma((total,)), dma((total,)), dma((total,)), dma((total,)),
         ],
         compiler_params=pltpu.CompilerParams(
-            collective_id=2, has_side_effects=True, vmem_limit_bytes=VMEM_LIMIT
+            collective_id=1, has_side_effects=True, vmem_limit_bytes=VMEM_LIMIT
         ),
-    )(residual, table, send_rows, send_ids)
+    )(hidden_full, table, target, send_rows, send_ids)
     return reduces, results
 
 
@@ -352,28 +402,13 @@
     block_width = model_width // n_d
 
     pieces, blocks = gather(hidden, n_d, n_v)
-    hidden_full = jnp.transpose(pieces, (1, 0, 2)).reshape(tokens, model_width)
-    hidden_block = jnp.transpose(blocks, (0, 2, 1, 3)).reshape(n_d * tokens, block_width)
-
-    logits = lax.dot_general(
-        hidden_full, table, (((1,), (1,)), ((), ())), preferred_element_type=jnp.float32
-    )
-    columns = lax.broadcasted_iota(jnp.int32, logits.shape, 1)
-    is_target = columns == (targets - first_row)[:, None]
-    picked = jnp.sum(jnp.where(is_target, logits, 0.0), axis=1)
-    local_max = jnp.max(logits, axis=1)
-    shifted = jnp.exp(logits - local_max[:, None])
-    local_sum = jnp.sum(shifted, axis=1)
-    stats = jnp.stack([local_max, local_sum, picked] + [picked] * 5)
-    shared = exchange_stats(stats, n_v)
-    maxima, sums = shared[:, 0], shared[:, 1]
-    row_max = jnp.max(maxima, axis=0)
-    row_sum = jnp.sum(sums * jnp.exp(maxima - row_max[None, :]), axis=0)
-    target_logit = jnp.sum(shared[:, 2], axis=0)
-    token_loss = row_max + jnp.log(row_sum) - target_logit
-    residual = (
-        jnp.exp(logits - row_max[:, None]) / row_sum[:, None] - jnp.where(is_target, 1.0, 0.0)
-    ).astype(jnp.bfloat16)
+    if hidden.shape[1] % 128 == 0:
+        hidden_full = pieces
+        hidden_block = blocks.reshape(n_d * tokens, block_width)
+    else:
+        hidden_full = jnp.transpose(pieces, (1, 0, 2)).reshape(tokens, model_width)
+        hidden_block = jnp.transpose(blocks, (0, 2, 1, 3)).reshape(n_d * tokens, block_width)
+    target = (targets - first_row)[:, None]
 
     row_count = input_ids.shape[0]
     capacity = max(2, 2 * row_count // n_v)
@@ -396,12 +431,13 @@
         constant_values=-1,
     )
 
-    reduces, (grad, res_all, got_rows, got_ids) = finish(
-        residual, table, send_rows, send_ids, n_d, n_v
+    reduces, (loss, grad, res_all, got_rows, got_ids) = finish(
+        hidden_full, table, target, send_rows, send_ids, n_d, n_v
     )
     if reduces:
         hidden_grad = grad
     else:
+        residual = lax.dynamic_index_in_dim(res_all, lax.axis_index("dp"), 0, keepdims=False)
         hidden_part = jnp.dot(residual, table, preferred_element_type=jnp.float32)
         hidden_grad = lax.psum_scatter(
             hidden_part, "vocab", scatter_dimension=1, tiled=True
@@ -420,7 +456,7 @@
         (((0,), (0,)), ((), ())),
         preferred_element_type=jnp.float32,
     )
-    return (token_loss, hidden_grad, table_sum.astype(jnp.bfloat16))
+    return (loss[0], hidden_grad, table_sum.astype(jnp.bfloat16))
 
 
 def solution(mesh):

time: 113 us -> 96.7 us (0.86)
  matrix products: 12.2 us -> 6.67 us
  local copies, waits for them, and re-layouts: 9.85 us -> 5.04 us
  other arithmetic: 5.71 us -> 1.68 us
  Pallas kernels: 84 us -> 82.3 us
    pallas_call x1 -> x0, Pallas kernels: 13.6 us -> none  [exchange_stats(): pl.pallas_call(functools.partial(stats_kernel, n_v), out_shape=jax.ShapeD...]
    pallas_call x1, Pallas kernels: 44.2 us -> 56.1 us  [finish(): pl.pallas_call(functools.partial(final_kernel, n_d, n_v, reduces), out_sh...]
    dot_general x1 -> x0, matrix products: 5.74 us -> none  [body(): lax.dot_general(hidden_full, table, (((1,), (1,)), ((), ())), preferred_e...]
    transpose x2 -> x0, local copies, waits for them, and re-layouts: 2.65 us -> none  [the longest x1 1.56 us: body(): hidden_full = jnp.transpose(pieces, (1, 0, 2)).reshape(tokens, model_width)]
    dot_general x1 -> x0, local copies, waits for them, and re-layouts: 1.91 us -> none  [body(): lax.dot_general(hidden_full, table, (((1,), (1,)), ((), ())), preferred_e...]
    convert_element_type x1 -> x0, other arithmetic: 1.69 us -> none  [body(): residual = (jnp.exp(logits - row_max[:, None]) / row_sum[:, None] - jnp.w...]
where the time goes in v2:
time: 96.7 us; the launch traced here: 96.4 us
  Pallas kernels  82.3 us (85%)
  matrix products  6.67 us (7%)
  local copies, waits for them, and re-layouts  5.04 us (5%)
  other arithmetic  1.68 us (2%)
    pallas_call x1, Pallas kernels, finish(): pl.pallas_call(functools.partial(final_kernel, n_d, n_v, reduces), out_sh...  56.1 us
    pallas_call x1, Pallas kernels, gather(): pl.pallas_call(functools.partial(gather_kernel, n_d, n_v), out_shape=(jax...  26.2 us
    dot_general x1, matrix products, body(): lax.dot_general(res_all.reshape(n_d * tokens, vocab_rows), hidden_block,...  3.84 us
    dot_general x1, matrix products, body(): jnp.dot(matches.astype(jnp.bfloat16), flat_rows, preferred_element_type=j...  2.43 us

profile of v2, /device:TPU:0, one launch (start us, length us, event | category | flops | bytes accessed | tf_op | source)
XLA Modules:
  0.0 96.4 jit_solution(1216569251694412294)
XLA Ops:
  0.6 0.0 copy-start
  0.6 0.7 broadcast_subtract_fusion
  1.4 0.7 subtract_add_fusion
  2.0 0.2 convert_reduce_fusion
  2.2 0.1 select_reduce_fusion
  2.3 0.1 sub.26
  2.4 0.6 pad.4.ids_ref
  3.0 0.8 copy.16.target_ref
  3.8 0.0 copy-done
  3.8 0.4 convolution_convert_fusion
  4.2 0.4 reshape.33
  4.6 0.9 copy.20
  5.5 26.2 %shard_map.76 = (bf16[256,2048]{1,0:T(8,128)(2,1)}, bf16[4,256,512]{2,1,0:T(8,128)(2,1)}) custom-call(bf16[256,256]{1,0:T(8,128)(2,1)} %own_ref.1), custom_call_target="tpu_custom_call" | custom-call | tf_op jit(solution)/shard_map/pallas_call | solution.py:145
  31.7 56.1 %shard_map.77 = (f32[1,256]{1,0:T(1,128)}, bf16[256,256]{1,0:T(8,128)(2,1)}, bf16[4,256,2000]{2,1,0:T(8,128)(2,1)}, bf16[4,8,16,512]{3,2,1,0:T(8,128)(2,1)}, s32[4,8,1,128]{3,2,1,0:T(1,128)}) custom-call(bf16[256,2048]{1,0:T(8,128)(2,1)} %get-tuple-element.10.hid_ref, bf16[2000,2048]{1,0:T(8,128)(2,1)} %table_ref.1, s32[256,1]{1,0:T(8,128)} %copy.16.target_ref, ...), custom_call_target="tpu_custom_call" | custom-call | tf_op jit(solution)/shard_map/pallas_call | solution.py:360
  87.9 0.8 slice_reduce_fusion
  88.6 0.1 eq.36
  88.7 0.0 copy-start.3
  88.7 0.0 copy-start.4
  88.7 2.4 %fusion.1 = f32[2000,512]{1,0:T(8,128)S(1)} fusion(bf16[512,512]{1,0:T(8,128)(2,1)} %bitcast.19, s32[512]{0:T(512)S(1)} %eq.36), kind=kOutput, calls=%fused_computation.3 | convolution fusion | flops 1049600000 | bytes 4622336 | tf_op jit(solution)/shard_map/dot_general | solution.py:452
  91.1 0.0 copy-done.3
  91.2 0.2 copy-done.4
  91.4 0.0 copy-start.2
  91.4 0.0 copy-start.1
  91.4 3.8 %fusion = bf16[2000,512]{1,0:T(8,128)(2,1)} fusion(f32[2000,512]{1,0:T(8,128)S(1)} %fusion.1, bf16[4,256,2000]{2,1,0:T(8,128)(2,1)S(1)} %copy-done.3, bf16[4,256,512]{2,1,0:T(8,128)(2,1)S(1)} %copy-done.4), kind=kOutput, calls=%fused_computation.1 | convolution fusion | flops 2099200000 | bytes 11288576 | tf_op jit(solution)/shard_map/dot_general | solution.py:453
  95.2 0.0 copy-done.2
  95.2 0.6 copy.23
  95.8 0.0 copy-done.1
  95.8 0.7 copy.24
  (2 shorter events, 0.0 us)
Async XLA Ops:
  0.6 3.2 %copy-start = (bf16[64,2048]{1,0:T(8,128)(2,1)S(1)}, bf16[64,2048]{1,0:T(8,128)(2,1)}, u32[]{:S(2)}) copy-start(bf16[64,2048]{1,0:T(8,128)(2,1)} %param.9) | copy-start | bytes 786436
  88.7 2.4 %copy-start.3 = (bf16[4,256,2000]{2,1,0:T(8,128)(2,1)S(1)}, bf16[4,256,2000]{2,1,0:T(8,128)(2,1)}, u32[]{:S(2)}) copy-start(bf16[4,256,2000]{2,1,0:T(8,128)(2,1)} %get-tuple-element.15) | copy-start | bytes 12288004
  88.7 2.6 %copy-start.4 = (bf16[4,256,512]{2,1,0:T(8,128)(2,1)S(1)}, bf16[4,256,512]{2,1,0:T(8,128)(2,1)}, u32[]{:S(2)}) copy-start(bf16[4,256,512]{2,1,0:T(8,128)(2,1)} %get-tuple-element.16) | copy-start | bytes 3145732
  91.4 3.8 %copy-start.2 = (f32[1,256]{1,0:T(1,128)S(1)}, f32[1,256]{1,0:T(1,128)}, u32[]{:S(2)}) copy-start(f32[1,256]{1,0:T(1,128)} %get-tuple-element.11) | copy-start | bytes 3076
  91.4 4.4 %copy-start.1 = (bf16[256,256]{1,0:T(8,128)(2,1)S(1)}, bf16[256,256]{1,0:T(8,128)(2,1)}, u32[]{:S(2)}) copy-start(bf16[256,256]{1,0:T(8,128)(2,1)} %get-tuple-element.23) | copy-start | bytes 393220
